TPU v7x, 32 devices: a whole 2x2x4 slice. The times are simulated.
32 devices in a mesh: parts: 2 (over x), space: 16 (over z, y, core).
Axes of the slice: x: 2, y: 2, z: 4, core: 2. Of those that a mesh axis runs over, the one named last changes fastest.
Arguments:
- state: float32 [66, 64, 8, 256], P('parts', 'space'), parts along dimension 0, may hold values from 0.25 to 6.5
- adjoint: float32 [64, 64, 8, 256], P('parts', 'space'), parts along dimension 0, may hold values from -6 to 6
- control: float32 [64, 64, 8, 256], P('parts', 'space'), parts along dimension 0, may hold values from -6 to 6
- target: float32 [64, 128], P('parts'), parts along dimension 0, may hold values from 1 to 3
- mask: int32 [64, 16], P('space', 'parts'), parts along dimension 1, may hold values 0 or 1
- regions: int32 [64, 16, 256], P('space', 'parts'), parts along dimension 1, may hold values from 0 to 127, as said below
Outputs:
- state_spectrum: float32 [2, 64, 64, 8, 256], P(None, 'parts', 'space'), parts along dimension 1
- adjoint_spectrum: float32 [2, 64, 64, 8, 256], P(None, 'parts', 'space'), parts along dimension 1
- gradient_residual: float32 [64, 64, 8, 256], P('parts', 'space'), parts along dimension 0
There are 2 independent parts, one for each index of `parts`. A program takes and returns all parts, laid end to end along the dimension named above; each array names one. Nothing has to cross between parts.
Inputs may be any that keep to these rules, and one draw needn't show every extreme that they name: `regions`: every region number from 0 to 127 labels at least one cell.
All inputs are finite; a program needn't handle non-finite values. No bound on the sum of `mask` on one device may be relied on, other than what follows from the above.
Results may differ from a plain program's by a relative error of at most 0.000098.
Values sent between devices are 32-bit elements; how exact they have to be, the bound alone decides.
A program may use at most 64 MiB of HBM per device.

v0:
```python
import math

import jax
import jax.numpy as jnp
from jax import lax
from jax.sharding import PartitionSpec as P

time_step = 0.15
penalty = 0.5


def with_halo(shard, sides, width):
    for axis, dim in sides:
        count, length = (lax.axis_size(axis), shard.shape[dim])
        up = [(i, (i + 1) % count) for i in range(count)]
        down = [(j, i) for i, j in up]
        last = lax.slice_in_dim(shard, length - width, length, axis=dim)
        initial = lax.slice_in_dim(shard, 0, width, axis=dim)
        before = lax.ppermute(last, axis, up)
        after = lax.ppermute(initial, axis, down)
        shard = jnp.concatenate([before, shard, after], axis=dim)
    return shard


def in_plane(values):
    padded = jnp.pad(values, ((0, 0), (0, 0), (1, 1), (1, 1)))
    across = padded[:, :, 2:, 1:-1] + padded[:, :, :-2, 1:-1]
    across = across + padded[:, :, 1:-1, 2:] + padded[:, :, 1:-1, :-2]
    return across - 6.0 * values


def spectrum(fourier, residual):
    count_steps = residual.shape[0]
    flattened = residual.reshape(count_steps, -1)
    result = jnp.dot(
        fourier, flattened, precision=lax.Precision.HIGHEST, preferred_element_type=jnp.float32
    )
    return result.reshape((2,) + residual.shape)


def on_device(state, adjoint, control, target, mask, regions):
    count_steps = control.shape[0]
    count_regions = target.shape[1]
    support = mask.astype(jnp.float32)[None, :, :, None]
    earlier = state[:-1]
    advanced = state[1:]
    following = adjoint[1:]
    state_wide = with_halo(earlier, (("space", 1),), 1)
    adjoint_wide = with_halo(following, (("space", 1),), 1)
    state_lap = in_plane(earlier) + state_wide[:, 2:] + state_wide[:, :-2]
    adjoint_lap = in_plane(following) + adjoint_wide[:, 2:] + adjoint_wide[:, :-2]
    state_res = advanced - earlier - time_step * state_lap - time_step * support * control
    flattened = advanced.reshape(count_steps, -1)
    region_ids = regions.reshape(-1)
    onehot = (region_ids[:, None] == jnp.arange(count_regions, dtype=jnp.int32)[None, :]).astype(
        jnp.float32
    )
    region_sums = jnp.dot(
        flattened, onehot, precision=lax.Precision.HIGHEST, preferred_element_type=jnp.float32
    )
    counts = jnp.sum(onehot, axis=0)
    region_sums, counts = lax.psum((region_sums, counts), "space")
    misfit = region_sums / counts - target
    source = lax.dot_general(
        misfit,
        onehot,
        (((1,), (1,)), ((), ())),
        precision=lax.Precision.HIGHEST,
        preferred_element_type=jnp.float32,
    )
    source = source.reshape(advanced.shape)
    adjoint_res = adjoint + source
    adjoint_res = adjoint_res.at[:-1].add(-(following + time_step * adjoint_lap))
    gradient_residual = penalty * control - support * adjoint
    indices = jnp.arange(count_steps, dtype=jnp.int32)
    phases = (
        2.0
        * math.pi
        / count_steps
        * (indices[:, None] * indices[None, :] % count_steps).astype(jnp.float32)
    )
    fourier = jnp.concatenate([jnp.cos(phases), -jnp.sin(phases)], 0)
    return (spectrum(fourier, state_res), spectrum(fourier, adjoint_res), gradient_residual)


def solution(mesh):
    return jax.shard_map(
        on_device,
        mesh=mesh,
        in_specs=(
            P("parts", "space", None, None),
            P("parts", "space", None, None),
            P("parts", "space", None, None),
            P("parts", None),
            P("space", "parts"),
            P("space", "parts", None),
        ),
        out_specs=(
            P(None, "parts", "space", None, None),
            P(None, "parts", "space", None, None),
            P("parts", "space", None, None),
        ),
        check_vma=False,
    )
```

profile of v0, /device:TPU:0, one launch (start us, length us, event | category | flops | bytes accessed | tf_op | source)
XLA Modules:
  0.0 100.0 jit_solution(15054435044258438798)
XLA Ops:
  0.6 0.0 copy-start.3
  0.6 1.1 %fusion.43 = (f32[31,1,8,256]{3,2,1,0:T(8,128)S(1)}, f32[31,1,8,256]{3,2,1,0:T(8,128)S(1)}) fusion(f32[32,4,8,256]{3,2,1,0:T(8,128)} %param.9), kind=kLoop, calls=%fused_computation.64 | loop fusion | bytes 1015808 | tf_op jit(solution)/shard_map/slice | solution.py:18
  1.8 5.5 %collective-permute-start.2 = (f32[31,1,8,256]{3,2,1,0:T(8,128)S(1)}, f32[31,1,8,256]{3,2,1,0:T(8,128)S(1)}, u32[]{:S(2)}, u32[]{:S(2)}) collective-permute-start(f32[31,1,8,256]{3,2,1,0:T(8,128)S(1)} %get-tuple-element.31), channel_id=1, source_target_pairs={{1,0},{2,1},{3,2},{4,3},{5,4},{6,5},{7,6},{8,7},{9,8},{10,9},{11,1... | collective-permute-start | bytes 761864 | tf_op jit(solution)/shard_map/ppermute | solution.py:20
  7.3 0.0 collective-permute-start.3
  7.3 1.1 %fusion.42 = (f32[32,1,8,256]{3,2,1,0:T(8,128)S(1)}, f32[32,1,8,256]{3,2,1,0:T(8,128)S(1)}) fusion(f32[33,4,8,256]{3,2,1,0:T(8,128)} %param.8), kind=kLoop, calls=%fused_computation.63 | loop fusion | bytes 1048576 | tf_op jit(solution)/shard_map/slice | solution.py:18
  8.4 4.5 %collective-permute-start = (f32[32,1,8,256]{3,2,1,0:T(8,128)S(1)}, f32[32,1,8,256]{3,2,1,0:T(8,128)S(1)}, u32[]{:S(2)}, u32[]{:S(2)}) collective-permute-start(f32[32,1,8,256]{3,2,1,0:T(8,128)S(1)} %get-tuple-element.28), channel_id=1, source_target_pairs={{1,0},{2,1},{3,2},{4,3},{5,4},{6,5},{7,6},{8,7},{9,8},{10,9},{11,1... | collective-permute-start | bytes 786440 | tf_op jit(solution)/shard_map/ppermute | solution.py:20
  12.8 0.0 collective-permute-start.1
  12.8 0.1 sine_negate_fusion
  12.9 0.0 copy-done.3
  12.9 0.0 copy-start.2
  13.0 3.7 %convert_reduce_fusion = f32[128]{0:T(128)S(1)} fusion(s32[8192]{0:T(1024)S(1)} %bitcast.54), kind=kLoop, calls=%fused_computation.8 | loop fusion | flops 3145600 | bytes 33280 | tf_op jit(solution)/shard_map/reduce_sum | solution.py:61
  16.7 0.0 copy-start.4
  16.7 0.0 copy-start
  16.7 0.0 copy-start.1
  16.7 0.0 slice-start.1
  16.8 0.6 copy-done.4
  17.4 0.0 collective-permute-done
  17.4 3.9 %collective-permute-done.1 = f32[32,1,8,256]{3,2,1,0:T(8,128)S(1)} collective-permute-done((f32[32,1,8,256]{3,2,1,0:T(8,128)S(1)}, f32[32,1,8,256]{3,2,1,0:T(8,128)S(1)}, u32[]{:S(2)}, u32[]{:S(2)}) %collective-permute-start.1) | collective-permute-done | bytes 262176 | tf_op jit(solution)/shard_map/ppermute | solution.py:19
  21.3 0.0 copy-done.2
  21.3 0.0 copy-done
  21.3 0.0 copy-done.1
  21.3 0.0 slice-done.1
  21.4 1.9 %fusion.41 = (f32[32,4,8,256]{3,2,1,0:T(8,128)S(1)}, f32[32,4,8,256]{3,2,1,0:T(8,128)S(1)}, f32[32,4,8,256]{3,2,1,0:T(8,128)}) fusion(f32[33,4,8,256]{3,2,1,0:T(8,128)S(1)} %copy-done.1, f32[32,4,8,256]{3,2,1,0:T(8,128)S(1)} %copy-done.2, f32[4,8]{1,0:T(4,128)S(1)} %broadcast_multiply_fusion, f32[32,4,8,256]{3,2,1,0:T(8,128)S(1)} %slice-done.1, ...), kind=kLoop, calls=%fused_computation.62 | loop fusion | flops 4456448 | bytes 7864576 | tf_op jit(solution)/shard_map/slice | solution.py:46
  23.2 0.0 copy-start.5
  23.2 0.6 copy.23
  23.8 1.8 %fusion.4 = f32[32,128]{1,0:T(8,128)S(1)} fusion(f32[32,8192]{1,0:T(8,128)S(1)} %bitcast.51, s32[8192]{0:T(1024)S(1)} %bitcast.55), kind=kOutput, calls=%fused_computation.14 | convolution fusion | flops 403701760 | bytes 1097728 | tf_op jit(solution)/shard_map/dot_general | solution.py:58
  25.6 59.2 %all-reduce.2 = (f32[32,128]{1,0:T(8,128)S(1)}, f32[128]{0:T(128)S(1)}) all-reduce(f32[32,128]{1,0:T(8,128)S(1)} %fusion.4, f32[128]{0:T(128)S(1)} %convert_reduce_fusion), channel_id=1, replica_groups=mesh['parts'=2,'space'=16] {'space'}, use_global_device_ids=true, to_apply=%region_0.1 | all-reduce | flops 4224 | bytes 33792 | tf_op jit(solution)/shard_map/psum | solution.py:62
  84.9 0.0 copy-done.5
  84.9 2.7 %fusion = f32[32,8192]{1,0:T(8,128)S(1)} fusion(s32[8192]{0:T(1024)S(1)} %bitcast.56, f32[32,128]{1,0:T(8,128)S(1)} %copy-done.5, f32[32,128]{1,0:T(8,128)S(1)} %get-tuple-element.24, f32[128]{0:T(128)S(1)} %get-tuple-element.25), kind=kOutput, calls=%fused_computation.10 | convolution fusion | flops 403709952 | bytes 1114624 | tf_op jit(solution)/shard_map/dot_general | solution.py:64
  87.6 0.3 copy.24
  87.9 0.0 slice-start
  87.9 0.2 add.65
  88.1 0.0 collective-permute-done.2
  88.1 0.0 collective-permute-done.3
  88.1 1.0 %slice-done = f32[31,4,8,256]{3,2,1,0:T(8,128)S(1)} async-done(((f32[32,4,8,256]{3,2,1,0:T(8,128)}), f32[31,4,8,256]{3,2,1,0:T(8,128)S(1)}, s32[]{:S(2)}) %slice-start) | async-done | bytes 1015832 | tf_op jit(solution)/shard_map/slice | solution.py:47
  89.2 1.1 %fusion.30 = f32[32,4,8,256]{3,2,1,0:T(8,128)S(1)} fusion(f32[32,4,8,256]{3,2,1,0:T(8,128)S(1)} %add.65, f32[31,4,8,256]{3,2,1,0:T(8,128)S(1)} %slice-done, f32[31,1,8,256]{3,2,1,0:T(8,128)S(1)} %collective-permute-done.3, f32[31,1,8,256]{3,2,1,0:T(8,128)S(1)} %collective-permute-done.2), kind=kLoop, calls=%fused_computation.43 | loop fusion | flops 3301376 | bytes 3555328 | tf_op jit(solution)/shard_map/scatter-add | solution.py:73
  90.3 2.3 %fusion.14 = f32[2,32,4,8,256]{4,1,3,2,0:T(8,128)S(1)} fusion(f32[2,32,32,1,1]{2,1,4,3,0:T(8,128)S(1)} %bitcast.52, f32[4,8,256,32]{2,1,0,3:T(8,128)S(1)} %bitcast.46), kind=kOutput, calls=%fused_computation.26 | convolution fusion | flops 201326592 | bytes 3153920 | tf_op jit(solution)/shard_map/dot_general | solution.py:35
  92.6 2.5 %copy.18 = f32[2,32,4,8,256]{4,3,2,1,0:T(8,128)} copy(f32[2,32,4,8,256]{4,1,3,2,0:T(8,128)S(1)} %fusion.14) | data formatting | bytes 4194304
  95.1 2.3 %fusion.16 = f32[2,32,4,8,256]{4,1,3,2,0:T(8,128)S(1)} fusion(f32[2,32,32,1,1]{2,1,4,3,0:T(8,128)S(1)} %bitcast.53, f32[4,8,256,32]{2,1,0,3:T(8,128)S(1)} %bitcast.47), kind=kOutput, calls=%fused_computation.28 | convolution fusion | flops 201326592 | bytes 3153920 | tf_op jit(solution)/shard_map/dot_general | solution.py:35
  97.5 2.5 %copy.17 = f32[2,32,4,8,256]{4,3,2,1,0:T(8,128)} copy(f32[2,32,4,8,256]{4,1,3,2,0:T(8,128)S(1)} %fusion.16) | data formatting | bytes 4194304
  (4 shorter events, 0.0 us)
Async XLA Ops:
  0.6 12.3 %copy-start.3 = (s32[4,8,256]{2,1,0:T(8,128)S(1)}, s32[4,8,256]{2,1,0:T(8,128)}, u32[]{:S(2)}) copy-start(s32[4,8,256]{2,1,0:T(8,128)} %param.13) | copy-start | bytes 98308
  1.8 86.4 %collective-permute-start.2 = (f32[31,1,8,256]{3,2,1,0:T(8,128)S(1)}, f32[31,1,8,256]{3,2,1,0:T(8,128)S(1)}, u32[]{:S(2)}, u32[]{:S(2)}) collective-permute-start(f32[31,1,8,256]{3,2,1,0:T(8,128)S(1)} %get-tuple-element.31), channel_id=1, source_target_pairs={{1,0},{2,1},{3,2},{4,3},{5,4},{6,5},{7,6},{8,7},{9,8},{10,9},{11,1... | collective-permute-start | bytes 761864 | tf_op jit(solution)/shard_map/ppermute | solution.py:20
  7.3 80.8 %collective-permute-start.3 = (f32[31,1,8,256]{3,2,1,0:T(8,128)S(1)}, f32[31,1,8,256]{3,2,1,0:T(8,128)S(1)}, u32[]{:S(2)}, u32[]{:S(2)}) collective-permute-start(f32[31,1,8,256]{3,2,1,0:T(8,128)S(1)} %get-tuple-element.32), channel_id=1, source_target_pairs={{0,1},{1,2},{2,3},{3,4},{4,5},{5,6},{6,7},{7,8},{8,9},{9,10},{10,1... | collective-permute-start | bytes 761864 | tf_op jit(solution)/shard_map/ppermute | solution.py:19
  8.4 9.1 %collective-permute-start = (f32[32,1,8,256]{3,2,1,0:T(8,128)S(1)}, f32[32,1,8,256]{3,2,1,0:T(8,128)S(1)}, u32[]{:S(2)}, u32[]{:S(2)}) collective-permute-start(f32[32,1,8,256]{3,2,1,0:T(8,128)S(1)} %get-tuple-element.28), channel_id=1, source_target_pairs={{1,0},{2,1},{3,2},{4,3},{5,4},{6,5},{7,6},{8,7},{9,8},{10,9},{11,1... | collective-permute-start | bytes 786440 | tf_op jit(solution)/shard_map/ppermute | solution.py:20
  12.8 8.5 %collective-permute-start.1 = (f32[32,1,8,256]{3,2,1,0:T(8,128)S(1)}, f32[32,1,8,256]{3,2,1,0:T(8,128)S(1)}, u32[]{:S(2)}, u32[]{:S(2)}) collective-permute-start(f32[32,1,8,256]{3,2,1,0:T(8,128)S(1)} %get-tuple-element.29), channel_id=1, source_target_pairs={{0,1},{1,2},{2,3},{3,4},{4,5},{5,6},{6,7},{7,8},{8,9},{9,10},{10,1... | collective-permute-start | bytes 786440 | tf_op jit(solution)/shard_map/ppermute | solution.py:19
  12.9 8.4 %copy-start.2 = (f32[32,4,8,256]{3,2,1,0:T(8,128)S(1)}, f32[32,4,8,256]{3,2,1,0:T(8,128)}, u32[]{:S(2)}) copy-start(f32[32,4,8,256]{3,2,1,0:T(8,128)} %param.10) | copy-start | bytes 3145732
  16.7 0.7 copy-start.4
  16.7 4.6 %copy-start = (f32[32,4,8,256]{3,2,1,0:T(8,128)S(1)}, f32[32,4,8,256]{3,2,1,0:T(8,128)}, u32[]{:S(2)}) copy-start(f32[32,4,8,256]{3,2,1,0:T(8,128)} %param.9) | copy-start | bytes 3145732
  16.7 4.6 %copy-start.1 = (f32[33,4,8,256]{3,2,1,0:T(8,128)S(1)}, f32[33,4,8,256]{3,2,1,0:T(8,128)}, u32[]{:S(2)}) copy-start(f32[33,4,8,256]{3,2,1,0:T(8,128)} %param.8) | copy-start | bytes 3244036
  16.7 4.6 %slice-start.1 = ((f32[33,4,8,256]{3,2,1,0:T(8,128)}), f32[32,4,8,256]{3,2,1,0:T(8,128)S(1)}, s32[]{:S(2)}) async-start(f32[33,4,8,256]{3,2,1,0:T(8,128)} %param.8), calls=%async_computation.1 | async-start | bytes 2097152 | tf_op jit(solution)/shard_map/slice | solution.py:45
  23.2 61.7 %copy-start.5 = (f32[32,128]{1,0:T(8,128)S(1)}, f32[32,128]{1,0:T(8,128)}, u32[]{:S(2)}) copy-start(f32[32,128]{1,0:T(8,128)} %param.11) | copy-start | bytes 49156
  87.9 1.2 %slice-start = ((f32[32,4,8,256]{3,2,1,0:T(8,128)}), f32[31,4,8,256]{3,2,1,0:T(8,128)S(1)}, s32[]{:S(2)}) async-start(f32[32,4,8,256]{3,2,1,0:T(8,128)} %param.9), calls=%async_computation | async-start | bytes 2031616 | tf_op jit(solution)/shard_map/slice | solution.py:47
where the time goes:
time: 100 us
  blocking collectives  59.2 us (59%)
  starting transfers between devices  10 us (10%)
  local copies, waits for them, and re-layouts  9.88 us (10%)
  matrix products  9.18 us (9%)
  other arithmetic  6.94 us (7%)
  waiting for transfers between devices  3.94 us (4%)
    psum x1, blocking collectives, on_device(): region_sums, counts = lax.psum((region_sums, counts), 'space')  59.2 us
    ppermute x2, starting transfers between devices, with_halo(): after = lax.ppermute(initial, axis, down)  10 us
    unnamed x17, local copies, waits for them, and re-layouts  6.68 us
    dot_general x2, matrix products, spectrum(): jnp.dot(fourier, flattened, precision=lax.Precision.HIGHEST, preferred_el...  4.66 us
    ppermute x2, waiting for transfers between devices, with_halo(): before = lax.ppermute(last, axis, up)  3.94 us
    reduce_sum x1, other arithmetic, on_device(): counts = jnp.sum(onehot, axis=0)  3.72 us
    dot_general x1, matrix products, on_device(): lax.dot_general(misfit, onehot, (((1,), (1,)), ((), ())), precision=lax.P...  2.71 us
    slice x2, local copies, waits for them, and re-layouts, with_halo(): initial = lax.slice_in_dim(shard, 0, width, axis=dim)  2.18 us
  transfers between devices with their start and end apart: 4, of which 1 were waited for; matrix products, arithmetic and copies ran while one was open for 12% of the time, Pallas kernels for 0%

commit v1 on v0

v1 whole, which is shorter than its diff:
```python
import functools
import math

import jax
import jax.numpy as jnp
from jax import lax
from jax.experimental import pallas as pl
from jax.experimental.pallas import tpu as pltpu
from jax.sharding import PartitionSpec as P

time_step = 0.15
penalty = 0.5
MESH = pl.DeviceIdType.MESH
ANY = pl.BlockSpec(memory_space=pl.ANY)


def pieces(length, parts):
    step = -(-length // parts)
    return [(start, min(step, length - start)) for start in range(0, length, step)]


def exchange_kernel(
    count, state, adjoint, regions, state_halo, adjoint_halo, totals,
    held, labels, partial, paired, summed, gathered,
    load_sem, halo_send, halo_recv, pair_send, pair_recv, peer_send, peer_recv,
):
    steps, rows, planes, width = (
        state.shape[0] - 1, state.shape[1], state.shape[2], state.shape[3],
    )
    count_regions = totals.shape[1]
    half = count // 2
    me = lax.axis_index("space")
    group, core = me // 2, me % 2
    above, below = (me + 1) % count, (me + count - 1) % count
    partner = group * 2 + 1 - core
    peers = [((group + d) % half) * 2 + core for d in range(1, half)]

    blocks = width // 128
    loads = [pltpu.make_async_copy(regions, labels, load_sem.at[blocks])] + [
        pltpu.make_async_copy(
            state.at[pl.ds(1, steps), :, :, pl.ds(block * 128, 128)], held.at[block], load_sem.at[block]
        )
        for block in range(blocks)
    ]
    for load in loads:
        load.start()
    barrier = pltpu.get_barrier_semaphore()
    for other in [above, below] + peers:
        pl.semaphore_signal(barrier, inc=1, device_id={"space": other}, device_id_type=MESH)
    pl.semaphore_wait(barrier, 1 + half)

    copies = []
    for source, first, target, length in ((state, 0, state_halo, steps), (adjoint, 1, adjoint_halo, steps - 1)):
        for start, size in pieces(length, 2):
            for side, (row, other) in enumerate(((rows - 1, above), (0, below))):
                n = len(copies)
                copies.append(
                    pltpu.make_async_remote_copy(
                        src_ref=source.at[pl.ds(first + start, size), row],
                        dst_ref=target.at[side, pl.ds(start, size)],
                        send_sem=halo_send.at[n],
                        recv_sem=halo_recv.at[n],
                        device_id={"space": other},
                        device_id_type=MESH,
                    )
                )
    for copy in copies[:2]:
        copy.start()

    for load in loads:
        load.wait()
    flat = held.reshape(blocks, steps * rows * planes, 128)
    region_ids = lax.broadcasted_iota(jnp.int32, (count_regions, width), 0)

    def add_row(row, total):
        values = jnp.concatenate(
            [
                flat[block, pl.ds(row * planes + plane, steps, stride=rows * planes), :]
                for plane in range(planes)
                for block in range(blocks)
            ],
            axis=1,
        )
        high = values.astype(jnp.bfloat16)
        low = (values - high.astype(jnp.float32)).astype(jnp.bfloat16)
        ones = jnp.ones((16, planes * width), jnp.bfloat16)
        stacked = jnp.concatenate([high, low, ones], axis=0)
        onehot = jnp.concatenate(
            [
                (labels[row, pl.ds(plane, 1), :] == region_ids).astype(jnp.float32).astype(jnp.bfloat16)
                for plane in range(planes)
            ],
            axis=1,
        )
        return total + lax.dot_general(
            stacked, onehot, (((1,), (1,)), ((), ())), preferred_element_type=jnp.float32
        )

    total = lax.fori_loop(
        0, rows, add_row, jnp.zeros((2 * steps + 16, count_regions), jnp.float32)
    )
    partial[:steps] = total[:steps] + total[steps : 2 * steps]
    partial[steps:] = total[2 * steps : 2 * steps + 8]
    pair = pltpu.make_async_remote_copy(
        src_ref=partial, dst_ref=paired, send_sem=pair_send.at[0], recv_sem=pair_recv.at[0],
        device_id={"space": partner}, device_id_type=MESH,
    )
    pair.start()
    pair.wait()
    summed[...] = partial[...] + paired[...]
    sends = [
        pltpu.make_async_remote_copy(
            src_ref=summed, dst_ref=gathered.at[d], send_sem=peer_send.at[d], recv_sem=peer_recv.at[d],
            device_id={"space": peer}, device_id_type=MESH,
        )
        for d, peer in enumerate(peers)
    ]
    for send in sends:
        send.start()
    for copy in copies[2:]:
        copy.start()
    result = summed[...]
    for d, send in enumerate(sends):
        send.wait()
        result = result + gathered[d]
    totals[...] = result
    for copy in copies:
        copy.wait()


def exchange(count, state, adjoint, regions, count_regions):
    levels, rows, planes, width = state.shape
    steps = levels - 1
    padded = (steps + 8, count_regions)
    half = count // 2
    f32 = jnp.float32
    return pl.pallas_call(
        functools.partial(exchange_kernel, count),
        out_shape=(
            jax.ShapeDtypeStruct((2, steps, planes, width), f32),
            jax.ShapeDtypeStruct((2, steps - 1, planes, width), f32),
            jax.ShapeDtypeStruct(padded, f32),
        ),
        in_specs=[ANY] * 3,
        out_specs=(ANY, ANY, pl.BlockSpec(memory_space=pltpu.VMEM)),
        scratch_shapes=[
            pltpu.VMEM((width // 128, steps, rows, planes, 128), f32),
            pltpu.VMEM(regions.shape, jnp.int32),
            pltpu.VMEM(padded, f32),
            pltpu.VMEM(padded, f32),
            pltpu.VMEM(padded, f32),
            pltpu.VMEM((half - 1,) + padded, f32),
            pltpu.SemaphoreType.DMA((width // 128 + 1,)),
            pltpu.SemaphoreType.DMA((8,)),
            pltpu.SemaphoreType.DMA((8,)),
            pltpu.SemaphoreType.DMA((1,)),
            pltpu.SemaphoreType.DMA((1,)),
            pltpu.SemaphoreType.DMA((half - 1,)),
            pltpu.SemaphoreType.DMA((half - 1,)),
        ],
        compiler_params=pltpu.CompilerParams(collective_id=0, has_side_effects=True),
        name="exchange",
    )(state, adjoint, regions)


def times(value, scale):
    if scale == 1.0:
        return value
    if scale == -1.0:
        return -value
    return value * scale


def real_transform(values):
    n = len(values)
    if n == 1:
        return [values[0]], [None]
    if n % 2:
        real, imag = [], []
        for k in range(n // 2 + 1):
            angles = [2.0 * math.pi * (j * k % n) / n for j in range(n)]
            real.append(sum(v * math.cos(a) for v, a in zip(values, angles)))
            imag.append(None if k == 0 else sum(v * -math.sin(a) for v, a in zip(values, angles)))
        return real, imag
    even_re, even_im = real_transform(values[::2])
    odd_re, odd_im = real_transform(values[1::2])
    m = n // 2
    real, imag = [None] * (m + 1), [None] * (m + 1)
    for k in range(m // 2 + 1):
        a_re, a_im, b_re, b_im = even_re[k], even_im[k], odd_re[k], odd_im[k]
        if k == 0:
            real[0], real[m] = a_re + b_re, a_re - b_re
            continue
        if 2 * k == m:
            real[k], imag[k] = a_re, -b_re
            continue
        c, s = math.cos(2.0 * math.pi * k / n), math.sin(2.0 * math.pi * k / n)
        t_re, t_im = c * b_re + s * b_im, c * b_im - s * b_re
        real[k], imag[k] = a_re + t_re, a_im + t_im
        real[m - k], imag[m - k] = a_re - t_re, t_im - a_im
    return real, imag


def write_spectrum(buffer, row, lanes, real, imag, n):
    zero = jnp.zeros_like(real[0])
    for k in range(n):
        low = min(k, n - k)
        buffer[0, row, k, :, lanes] = real[low]
        value = imag[low]
        buffer[1, row, k, :, lanes] = zero if value is None else (value if k == low else -value)


def residual_kernel(
    state, adjoint, control, target, mask, regions, state_halo, adjoint_halo, totals,
    state_out, adjoint_out, gradient_out,
    held, multipliers, heat, labels, residual, table, misfits, state_buffer, adjoint_buffer, gradient,
    held_sem, mult_sem, heat_sem, label_sem, state_sem, adjoint_sem, gradient_sem,
):
    steps, rows, planes, width = control.shape
    lane_blocks = width // 128

    def state_row(y):
        source = state_halo.at[0] if y < 0 else state_halo.at[1] if y == rows else state.at[pl.ds(0, steps + 1), y]
        into = held.at[y + 1, pl.ds(0, steps)] if y < 0 or y == rows else held.at[y + 1]
        return pltpu.make_async_copy(source, into, held_sem.at[y + 1])

    def adjoint_row(y):
        source = adjoint_halo.at[0] if y < 0 else adjoint_halo.at[1] if y == rows else adjoint.at[pl.ds(0, steps), y]
        into = multipliers.at[y + 1, pl.ds(1, steps - 1)] if y < 0 or y == rows else multipliers.at[y + 1]
        return pltpu.make_async_copy(source, into, mult_sem.at[y + 1])

    control_rows = [
        pltpu.make_async_copy(control.at[pl.ds(0, steps), y], heat.at[y], heat_sem.at[y]) for y in range(rows)
    ]
    state_rows = {y: state_row(y) for y in range(-1, rows + 1)}
    adjoint_rows = {y: adjoint_row(y) for y in range(-1, rows + 1)}
    label_copy = pltpu.make_async_copy(regions, labels, label_sem.at[0])
    label_copy.start()
    state_rows[-1].start()
    adjoint_rows[-1].start()
    state_rows[0].start()
    adjoint_rows[0].start()
    for y in range(rows):
        state_rows[y + 1].start()
        adjoint_rows[y + 1].start()
        control_rows[y].start()

    misfits[...] = totals[:steps] / totals[steps : steps + 1] - target[...]
    real, imag = real_transform(
        [jnp.broadcast_to(misfits[pl.ds(j, 1), :], (8, misfits.shape[1])) for j in range(steps)]
    )
    for k in range(steps // 2 + 1):
        table[k] = real[k]
        if imag[k] is not None:
            table[steps // 2 + k] = imag[k]
    label_copy.wait()

    lane = lax.broadcasted_iota(jnp.int32, (planes, width), 1)
    plane = lax.broadcasted_iota(jnp.int32, (planes, width), 0)
    first_lane, last_lane = lane == 0, lane == width - 1
    first_plane, last_plane = plane == 0, plane == planes - 1

    def laplace(values, before, after):
        total = before + after
        total = total + jnp.where(first_lane, 0.0, pltpu.roll(values, 1, 1))
        total = total + jnp.where(last_lane, 0.0, pltpu.roll(values, width - 1, 1))
        total = total + jnp.where(first_plane, 0.0, pltpu.roll(values, 1, 0))
        total = total + jnp.where(last_plane, 0.0, pltpu.roll(values, planes - 1, 0))
        return total - 6.0 * values

    state_rows[-1].wait()
    adjoint_rows[-1].wait()
    state_rows[0].wait()
    adjoint_rows[0].wait()

    def one_row(y):
        support = mask[y]

        def state_step(j, carry):
            now = held[y + 1, j]
            lap = laplace(now, held[y, j], held[y + 2, j])
            force = heat[y, j]
            residual[j] = held[y + 1, j + 1] - now - time_step * lap - time_step * support * force
            gradient[y, j] = penalty * force - support * multipliers[y + 1, j]
            return carry

        lax.fori_loop(0, steps, state_step, 0, unroll=8)
        for block in range(lane_blocks):
            lanes = pl.ds(block * 128, 128)
            real, imag = real_transform([residual[j, :, lanes] for j in range(steps)])
            write_spectrum(state_buffer, y, lanes, real, imag, steps)

        def adjoint_step(j, carry):
            later = multipliers[y + 1, j + 1]
            lap = laplace(later, multipliers[y, j + 1], multipliers[y + 2, j + 1])
            residual[j] = multipliers[y + 1, j] - later - time_step * lap
            return carry

        lax.fori_loop(0, steps - 1, adjoint_step, 0, unroll=8)
        residual[steps - 1] = multipliers[y + 1, steps - 1]
        for block in range(lane_blocks):
            lanes = pl.ds(block * 128, 128)
            ids = labels[y, :, lanes]
            real, imag = real_transform([residual[j, :, lanes] for j in range(steps)])

            def looked_up(k):
                return jnp.take_along_axis(table[k], ids, axis=1, mode="promise_in_bounds")

            real = [v + looked_up(k) for k, v in enumerate(real)]
            imag = [None if v is None else v + looked_up(steps // 2 + k) for k, v in enumerate(imag)]
            write_spectrum(adjoint_buffer, y, lanes, real, imag, steps)

    def outputs(y):
        found = [pltpu.make_async_copy(gradient.at[y], gradient_out.at[pl.ds(0, steps), y], gradient_sem.at[y])]
        for part in range(2):
            found.append(
                pltpu.make_async_copy(
                    state_buffer.at[part, y], state_out.at[part, pl.ds(0, steps), y], state_sem.at[part, y]
                )
            )
            found.append(
                pltpu.make_async_copy(
                    adjoint_buffer.at[part, y], adjoint_out.at[part, pl.ds(0, steps), y], adjoint_sem.at[part, y]
                )
            )
        return found

    def row_body(y, carry):
        for when in range(rows):
            @pl.when(y == when)
            def _():
                state_rows[when + 1].wait()
                adjoint_rows[when + 1].wait()
                control_rows[when].wait()

        one_row(y)
        for copy in outputs(y):
            copy.start()
        return carry

    lax.fori_loop(0, rows, row_body, 0)
    for y in range(rows):
        for copy in outputs(y):
            copy.wait()


def residuals(state, adjoint, control, target, support, regions, state_halo, adjoint_halo, totals):
    steps, rows, planes, width = control.shape
    f32 = jnp.float32
    vmem = pl.BlockSpec(memory_space=pltpu.VMEM)
    spectrum_shape = jax.ShapeDtypeStruct((2,) + control.shape, f32)
    dma = pltpu.SemaphoreType.DMA
    return pl.pallas_call(
        residual_kernel,
        out_shape=(spectrum_shape, spectrum_shape, jax.ShapeDtypeStruct(control.shape, f32)),
        in_specs=[ANY, ANY, ANY, vmem, vmem, ANY, ANY, ANY, vmem],
        out_specs=(ANY, ANY, ANY),
        scratch_shapes=[
            pltpu.VMEM((rows + 2, steps + 1, planes, width), f32),
            pltpu.VMEM((rows + 2, steps, planes, width), f32),
            pltpu.VMEM((rows, steps, planes, width), f32),
            pltpu.VMEM(regions.shape, jnp.int32),
            pltpu.VMEM((steps, planes, width), f32),
            pltpu.VMEM((steps, 8, target.shape[1]), f32),
            pltpu.VMEM(target.shape, f32),
            pltpu.VMEM((2, rows, steps, planes, width), f32),
            pltpu.VMEM((2, rows, steps, planes, width), f32),
            pltpu.VMEM((rows, steps, planes, width), f32),
            dma((rows + 2,)),
            dma((rows + 2,)),
            dma((rows,)),
            dma((1,)),
            dma((2, rows)),
            dma((2, rows)),
            dma((rows,)),
        ],
        name="residuals",
    )(state, adjoint, control, target, support, regions, state_halo, adjoint_halo, totals)


def on_device(count, state, adjoint, control, target, mask, regions):
    width = control.shape[3]
    support = jnp.broadcast_to(mask.astype(jnp.float32)[:, :, None], mask.shape + (width,))
    state_halo, adjoint_halo, totals = exchange(count, state, adjoint, regions, target.shape[1])
    return residuals(
        state, adjoint, control, target, support, regions, state_halo, adjoint_halo, totals
    )


def solution(mesh):
    return jax.shard_map(
        functools.partial(on_device, mesh.shape["space"]),
        mesh=mesh,
        in_specs=(
            P("parts", "space", None, None),
            P("parts", "space", None, None),
            P("parts", "space", None, None),
            P("parts", None),
            P("space", "parts"),
            P("space", "parts", None),
        ),
        out_specs=(
            P(None, "parts", "space", None, None),
            P(None, "parts", "space", None, None),
            P("parts", "space", None, None),
        ),
        check_vma=False,
    )
```

time: 100 us -> 33 us (0.33)
  the two profiles are of different devices: /device:TPU:0 before, /device:TPU:1 now
where the time goes in v1:
time: 33 us; the launch traced here: 32.8 us
  Pallas kernels  30.8 us (93%)
  other arithmetic  0.68 us (2%)
  local copies, waits for them, and re-layouts  0.67 us (2%)
  between operations  0.64 us (2%)
    pallas_call x1, Pallas kernels, exchange(): pl.pallas_call(functools.partial(exchange_kernel, count), out_shape=(jax....  20.8 us
    pallas_call x1, Pallas kernels, residuals(): pl.pallas_call(residual_kernel, out_shape=(spectrum_shape, spectrum_shape...  10.1 us
    convert_element_type x1, other arithmetic, on_device(): mask.astype(jnp.float32)[:, :, None]  0.68 us
    broadcast_in_dim x1, local copies, waits for them, and re-layouts, on_device(): jnp.broadcast_to(mask.astype(jnp.float32)[:, :, None], mask.shape + (widt...  0.67 us

profile of v1, /device:TPU:1, one launch (start us, length us, event | category | flops | bytes accessed | tf_op | source)
XLA Modules:
  0.0 32.8 jit_solution(4923895520888382456)
XLA Ops:
  0.6 0.7 %convert_element_type.3 = f32[4,8]{1,0:T(4,128)S(1)} convert(s32[4,8]{1,0:T(4,128)} %param.10) | non-fusion elementwise | flops 32 | bytes 256 | tf_op jit(solution)/shard_map/convert_element_type | solution.py:383
  1.3 0.7 %broadcast_in_dim.2.mask = f32[4,8,256]{2,1,0:T(8,128)} broadcast(f32[4,8]{1,0:T(4,128)S(1)} %convert_element_type.3), dimensions={0,1} | broadcast | bytes 32896 | tf_op jit(solution)/shard_map/broadcast_in_dim | solution.py:383
  2.0 20.8 %exchange.1 = (f32[2,32,8,256]{3,2,1,0:T(8,128)}, f32[2,31,8,256]{3,2,1,0:T(8,128)}, f32[40,128]{1,0:T(8,128)}) custom-call(f32[33,4,8,256]{3,2,1,0:T(8,128)} %state.3, f32[32,4,8,256]{3,2,1,0:T(8,128)} %adjoint.3, s32[4,8,256]{2,1,0:T(8,128)} %regions.3), custom_call_target="tpu_custom_call" | custom-call | tf_op jit(solution)/shard_map/exchange/pallas_call | solution.py:137
  22.8 10.1 %residuals.1 = (f32[2,32,4,8,256]{4,3,2,1,0:T(8,128)}, f32[2,32,4,8,256]{4,3,2,1,0:T(8,128)}, f32[32,4,8,256]{3,2,1,0:T(8,128)}) custom-call(f32[33,4,8,256]{3,2,1,0:T(8,128)} %state.3, f32[32,4,8,256]{3,2,1,0:T(8,128)} %adjoint.3, f32[32,4,8,256]{3,2,1,0:T(8,128)} %control.1, f32[32,128]{1,0:T(8,128)} %target.1, f32[4,8,256]{2,1,0:T(8,128)} %broadcast_in_dim.2.mask, ...), custom_call_target="tpu_custom_call" | custom-call | tf_op jit(solution)/shard_map/residuals/pallas_call | solution.py:353

commit v2 on v0

v2 whole, which is shorter than its diff:
```python
import functools
import math

import jax
import jax.numpy as jnp
from jax import lax
from jax.experimental import pallas as pl
from jax.experimental.pallas import tpu as pltpu
from jax.sharding import PartitionSpec as P

time_step = 0.15
penalty = 0.5
MESH = pl.DeviceIdType.MESH
ANY = pl.BlockSpec(memory_space=pl.ANY)


def real_transform(values):
    n = len(values)
    if n == 1:
        return [values[0]], [None]
    if n % 2:
        real, imag = [], []
        for k in range(n // 2 + 1):
            angles = [2.0 * math.pi * (j * k % n) / n for j in range(n)]
            real.append(sum(v * math.cos(a) for v, a in zip(values, angles)))
            imag.append(None if k == 0 else sum(v * -math.sin(a) for v, a in zip(values, angles)))
        return real, imag
    even_re, even_im = real_transform(values[::2])
    odd_re, odd_im = real_transform(values[1::2])
    m = n // 2
    real, imag = [None] * (m + 1), [None] * (m + 1)
    for k in range(m // 2 + 1):
        a_re, a_im, b_re, b_im = even_re[k], even_im[k], odd_re[k], odd_im[k]
        if k == 0:
            real[0], real[m] = a_re + b_re, a_re - b_re
            continue
        if 2 * k == m:
            real[k], imag[k] = a_re, -b_re
            continue
        c, s = math.cos(2.0 * math.pi * k / n), math.sin(2.0 * math.pi * k / n)
        t_re, t_im = c * b_re + s * b_im, c * b_im - s * b_re
        real[k], imag[k] = a_re + t_re, a_im + t_im
        real[m - k], imag[m - k] = a_re - t_re, t_im - a_im
    return real, imag


def write_spectrum(buffer, row, lanes, real, imag, n):
    zero = jnp.zeros_like(real[0])
    for k in range(n):
        low = min(k, n - k)
        buffer[0, row, k, :, lanes] = real[low]
        value = imag[low]
        buffer[1, row, k, :, lanes] = zero if value is None else (value if k == low else -value)


def pack(real, imag):
    return real + [value for value in imag if value is not None]


def solve_kernel(
    count, state, adjoint, control, regions, target, mask,
    state_buffer, packed, gradient, table,
    sampled, held, multipliers, heat, labels, residual, partial, paired, summed, gathered,
    label_sem, sample_sem, held_sem, mult_sem, heat_sem,
    halo_send, halo_recv, pair_send, pair_recv, peer_send, peer_recv,
):
    steps, rows, planes, width = control.shape
    count_regions = target.shape[1]
    blocks = width // 128
    half = count // 2
    me = lax.axis_index("space")
    group, core = me // 2, me % 2
    above, below = (me + 1) % count, (me + count - 1) % count
    partner = group * 2 + 1 - core
    peers = [((group + d) % half) * 2 + core for d in range(1, half)]

    barrier = pltpu.get_barrier_semaphore()
    for other in [above, below] + peers:
        pl.semaphore_signal(barrier, inc=1, device_id={"space": other}, device_id_type=MESH)

    sums_loads = [pltpu.make_async_copy(regions, labels, label_sem.at[0])] + [
        pltpu.make_async_copy(
            state.at[pl.ds(1, steps), :, :, pl.ds(block * 128, 128)],
            sampled.at[block], sample_sem.at[block],
        )
        for block in range(blocks)
    ]
    heat_loads, mult_loads, held_loads = [], [], []
    for y in range(rows):
        heat_loads.append(pltpu.make_async_copy(control.at[pl.ds(0, steps), y], heat.at[y], heat_sem.at[y]))
        mult_loads.append(
            pltpu.make_async_copy(adjoint.at[pl.ds(0, steps), y], multipliers.at[y + 1], mult_sem.at[y])
        )
        held_loads.append(
            pltpu.make_async_copy(state.at[pl.ds(0, steps + 1), y], held.at[y + 1], held_sem.at[y])
        )
    for load in sums_loads + heat_loads + mult_loads + held_loads:
        load.start()

    copies = []
    for source, first, target_rows, shift, length in (
        (state, 0, held, 0, steps), (adjoint, 1, multipliers, 1, steps - 1),
    ):
        for block in range(blocks):
            lanes = pl.ds(block * 128, 128)
            for row, into, other in ((rows - 1, 0, above), (0, rows + 1, below)):
                n = len(copies)
                copies.append(
                    pltpu.make_async_remote_copy(
                        src_ref=source.at[pl.ds(first, length), row, :, lanes],
                        dst_ref=target_rows.at[into, pl.ds(shift, length), :, lanes],
                        send_sem=halo_send.at[n],
                        recv_sem=halo_recv.at[n],
                        device_id={"space": other},
                        device_id_type=MESH,
                    )
                )

    flat = sampled.reshape(blocks, steps * rows * planes, 128)
    region_ids = lax.broadcasted_iota(jnp.int32, (count_regions, width), 0)

    def add_row(row, total):
        values = jnp.concatenate(
            [
                flat[block, pl.ds(row * planes + plane, steps, stride=rows * planes), :]
                for plane in range(planes)
                for block in range(blocks)
            ],
            axis=1,
        )
        high = values.astype(jnp.bfloat16)
        low = (values - high.astype(jnp.float32)).astype(jnp.bfloat16)
        ones = jnp.ones((16, planes * width), jnp.bfloat16)
        stacked = jnp.concatenate([high, low, ones], axis=0)
        onehot = jnp.concatenate(
            [
                (labels[row, pl.ds(plane, 1), :] == region_ids).astype(jnp.float32).astype(jnp.bfloat16)
                for plane in range(planes)
            ],
            axis=1,
        )
        return total + lax.dot_general(
            stacked, onehot, (((1,), (1,)), ((), ())), preferred_element_type=jnp.float32
        )

    for load in sums_loads:
        load.wait()
    early = rows // 2
    total = jnp.zeros((2 * steps + 16, count_regions), jnp.float32)
    total = lax.fori_loop(0, early, add_row, total)
    pl.semaphore_wait(barrier, 1 + half)
    for copy in copies[:2]:
        copy.start()
    total = lax.fori_loop(early, rows, add_row, total)
    partial[:steps] = total[:steps] + total[steps : 2 * steps]
    partial[steps:] = total[2 * steps : 2 * steps + 8]
    pair = pltpu.make_async_remote_copy(
        src_ref=partial, dst_ref=paired, send_sem=pair_send.at[0], recv_sem=pair_recv.at[0],
        device_id={"space": partner}, device_id_type=MESH,
    )
    pair.start()

    lane = lax.broadcasted_iota(jnp.int32, (planes, width), 1)
    plane_ids = lax.broadcasted_iota(jnp.int32, (planes, width), 0)
    first_lane, last_lane = lane == 0, lane == width - 1
    first_plane, last_plane = plane_ids == 0, plane_ids == planes - 1

    def support_of(y):
        support = jnp.zeros((planes, width), jnp.float32)
        for plane in range(planes):
            support = jnp.where(plane_ids == plane, mask[y, plane].astype(jnp.float32), support)
        return support

    for load in heat_loads + mult_loads:
        load.wait()

    def gradient_row(y, carry):
        support = support_of(y)

        def step(j, inner):
            gradient[y, j] = penalty * heat[y, j] - support * multipliers[y + 1, j]
            return inner

        return lax.fori_loop(0, steps, step, carry, unroll=8)

    lax.fori_loop(0, rows, gradient_row, 0)

    pair.wait()
    summed[...] = partial[...] + paired[...]
    sends = [
        pltpu.make_async_remote_copy(
            src_ref=summed, dst_ref=gathered.at[d], send_sem=peer_send.at[d], recv_sem=peer_recv.at[d],
            device_id={"space": peer}, device_id_type=MESH,
        )
        for d, peer in enumerate(peers)
    ]
    for send in sends:
        send.start()
    for copy in copies[2:]:
        copy.start()

    def laplace(values, beside):
        total = beside + jnp.where(first_lane, 0.0, pltpu.roll(values, 1, 1))
        total = total + jnp.where(last_lane, 0.0, pltpu.roll(values, width - 1, 1))
        total = total + jnp.where(first_plane, 0.0, pltpu.roll(values, 1, 0))
        total = total + jnp.where(last_plane, 0.0, pltpu.roll(values, planes - 1, 0))
        return total - 6.0 * values

    def adjoint_transform(y, beside):
        def step(j, carry):
            later = multipliers[y + 1, j + 1]
            residual[j] = multipliers[y + 1, j] - later - time_step * laplace(later, beside(j + 1))
            return carry

        lax.fori_loop(0, steps - 1, step, 0, unroll=8)
        residual[steps - 1] = multipliers[y + 1, steps - 1]
        for block in range(blocks):
            lanes = pl.ds(block * 128, 128)
            values = real_transform([residual[j, :, lanes] for j in range(steps)])
            for k, value in enumerate(pack(*values)):
                packed[y, k, :, lanes] = value

    def adjoint_inner(y, carry):
        adjoint_transform(y, lambda j: multipliers[y, j] + multipliers[y + 2, j])
        return carry

    def adjoint_edge(side, carry):
        adjoint_transform(side * (rows - 1), lambda j: multipliers[2 + side * (rows - 3), j])
        return carry

    def state_row(y, carry):
        support = support_of(y)

        def step(j, inner):
            now = held[y + 1, j]
            lap = laplace(now, held[y, j] + held[y + 2, j])
            residual[j] = held[y + 1, j + 1] - now - time_step * lap - time_step * support * heat[y, j]
            return inner

        lax.fori_loop(0, steps, step, 0, unroll=8)
        for block in range(blocks):
            lanes = pl.ds(block * 128, 128)
            real, imag = real_transform([residual[j, :, lanes] for j in range(steps)])
            write_spectrum(state_buffer, y, lanes, real, imag, steps)
        return carry

    lax.fori_loop(1, rows - 1, adjoint_inner, 0)
    lax.fori_loop(0, 2, adjoint_edge, 0)
    for load in held_loads:
        load.wait()
    lax.fori_loop(1, rows - 1, state_row, 0)
    for copy in copies[: 2 * blocks]:
        copy.wait()
    lax.fori_loop(0, 2, lambda side, carry: state_row(side * (rows - 1), carry), 0)

    result = summed[...]
    for d, send in enumerate(sends):
        send.wait()
        result = result + gathered[d]
    misfit = result[:steps] / result[steps : steps + 1] - target[...]
    values = real_transform(
        [jnp.broadcast_to(misfit[j : j + 1], (8, count_regions)) for j in range(steps)]
    )
    for k, value in enumerate(pack(*values)):
        table[k] = value

    for block in range(blocks):
        lanes = pl.ds(block * 128, 128)
        for side in range(2):
            copies[2 * (blocks + block) + side].wait()

        def add_halo(side, carry):
            y, outer = side * (rows - 1), side * (rows + 1)
            values = [-time_step * multipliers[outer, j + 1, :, lanes] for j in range(steps - 1)]
            values.append(jnp.zeros_like(values[0]))
            for k, value in enumerate(pack(*real_transform(values))):
                packed[y, k, :, lanes] += value
            return carry

        lax.fori_loop(0, 2, add_halo, 0)


def solve(count, state, adjoint, control, regions, target, mask):
    steps, rows, planes, width = control.shape
    count_regions = target.shape[1]
    padded = (steps + 8, count_regions)
    half, blocks = count // 2, width // 128
    f32, dma, vmem = jnp.float32, pltpu.SemaphoreType.DMA, pltpu.VMEM
    in_vmem = pl.BlockSpec(memory_space=pltpu.VMEM)
    return pl.pallas_call(
        functools.partial(solve_kernel, count),
        out_shape=(
            vmem((2, rows, steps, planes, width), f32),
            vmem((rows, steps, planes, width), f32),
            vmem((rows, steps, planes, width), f32),
            vmem((steps, 8, count_regions), f32),
        ),
        in_specs=[ANY] * 4 + [in_vmem, pl.BlockSpec(memory_space=pltpu.SMEM)],
        out_specs=(in_vmem,) * 4,
        scratch_shapes=[
            vmem((blocks, steps, rows, planes, 128), f32),
            vmem((rows + 2, steps + 1, planes, width), f32),
            vmem((rows + 2, steps, planes, width), f32),
            vmem((rows, steps, planes, width), f32),
            vmem(regions.shape, jnp.int32),
            vmem((steps, planes, width), f32),
            vmem(padded, f32),
            vmem(padded, f32),
            vmem(padded, f32),
            vmem((half - 1,) + padded, f32),
            dma((1,)),
            dma((blocks,)),
            dma((rows,)),
            dma((rows,)),
            dma((rows,)),
            dma((4 * blocks,)),
            dma((4 * blocks,)),
            dma((1,)),
            dma((1,)),
            dma((half - 1,)),
            dma((half - 1,)),
        ],
        compiler_params=pltpu.CompilerParams(
            collective_id=0, has_side_effects=True, vmem_limit_bytes=24 * 2**20
        ),
        name="solve",
    )(state, adjoint, control, regions, target, mask)


def finish_kernel(
    state_buffer, packed, gradient, table, labels,
    state_out, adjoint_out, gradient_out,
    adjoint_buffer, state_sem, adjoint_sem, gradient_sem,
):
    rows, steps, planes, width = gradient.shape
    early = []
    for y in range(rows):
        for part in range(2):
            early.append(
                pltpu.make_async_copy(
                    state_buffer.at[part, y], state_out.at[part, pl.ds(0, steps), y], state_sem.at[part, y]
                )
            )
        early.append(
            pltpu.make_async_copy(gradient.at[y], gradient_out.at[pl.ds(0, steps), y], gradient_sem.at[y])
        )
    for copy in early:
        copy.start()

    def outputs(y):
        return [
            pltpu.make_async_copy(
                adjoint_buffer.at[part, y], adjoint_out.at[part, pl.ds(0, steps), y], adjoint_sem.at[part, y]
            )
            for part in range(2)
        ]

    def row_body(y, carry):
        for block in range(width // 128):
            lanes = pl.ds(block * 128, 128)
            ids = labels[y, :, lanes]
            values = [
                packed[y, k, :, lanes] + jnp.take_along_axis(table[k], ids, axis=1, mode="promise_in_bounds")
                for k in range(steps)
            ]
            top = steps // 2 + 1
            imag = [None] + values[top:] + [None] * (2 * top - 1 - steps)
            write_spectrum(adjoint_buffer, y, lanes, values[:top], imag, steps)
        for copy in outputs(y):
            copy.start()
        return carry

    lax.fori_loop(0, rows, row_body, 0)
    for copy in early + [copy for y in range(rows) for copy in outputs(y)]:
        copy.wait()


def finish(control, state_buffer, packed, gradient, table, regions):
    steps, rows, planes, width = control.shape
    f32, dma = jnp.float32, pltpu.SemaphoreType.DMA
    in_vmem = pl.BlockSpec(memory_space=pltpu.VMEM)
    spectrum_shape = jax.ShapeDtypeStruct((2,) + control.shape, f32)
    return pl.pallas_call(
        finish_kernel,
        out_shape=(spectrum_shape, spectrum_shape, jax.ShapeDtypeStruct(control.shape, f32)),
        in_specs=[in_vmem] * 5,
        out_specs=(ANY,) * 3,
        scratch_shapes=[
            pltpu.VMEM((2, rows, steps, planes, width), f32),
            dma((2, rows)),
            dma((2, rows)),
            dma((rows,)),
        ],
        compiler_params=pltpu.CompilerParams(vmem_limit_bytes=16 * 2**20),
        name="finish",
    )(state_buffer, packed, gradient, table, regions)


def on_device(count, state, adjoint, control, target, mask, regions):
    found = solve(count, state, adjoint, control, regions, target, mask)
    return finish(control, *found, regions)


def solution(mesh):
    return jax.shard_map(
        functools.partial(on_device, mesh.shape["space"]),
        mesh=mesh,
        in_specs=(
            P("parts", "space", None, None),
            P("parts", "space", None, None),
            P("parts", "space", None, None),
            P("parts", None),
            P("space", "parts"),
            P("space", "parts", None),
        ),
        out_specs=(
            P(None, "parts", "space", None, None),
            P(None, "parts", "space", None, None),
            P("parts", "space", None, None),
        ),
        check_vma=False,
    )
```

time: 100 us -> 30.4 us (0.30)
  the two profiles are of different devices: /device:TPU:0 before, /device:TPU:1 now
where the time goes in v2:
time: 30.4 us; the launch traced here: 30 us
  Pallas kernels  23.5 us (77%)
  local copies, waits for them, and re-layouts  5.83 us (19%)
  between operations  0.65 us (2%)
    pallas_call x1, Pallas kernels, solve(): pl.pallas_call(functools.partial(solve_kernel, count), out_shape=(vmem((2...  21 us
    unnamed x12, local copies, waits for them, and re-layouts  5.83 us
    pallas_call x1, Pallas kernels, finish(): pl.pallas_call(finish_kernel, out_shape=(spectrum_shape, spectrum_shape,...  2.49 us

profile of v2, /device:TPU:1, one launch (start us, length us, event | category | flops | bytes accessed | tf_op | source)
XLA Modules:
  0.0 30.0 jit_solution(2966228100655302211)
XLA Ops:
  0.6 0.0 copy-start
  0.6 1.2 %copy-done = f32[33,4,8,256]{3,2,1,0:T(8,128)S(1)} copy-done((f32[33,4,8,256]{3,2,1,0:T(8,128)S(1)}, f32[33,4,8,256]{3,2,1,0:T(8,128)}, u32[]{:S(2)}) %copy-start) | copy-done | bytes 1081368
  1.9 0.0 copy-start.1
  1.9 1.2 %copy-done.1 = f32[32,4,8,256]{3,2,1,0:T(8,128)S(1)} copy-done((f32[32,4,8,256]{3,2,1,0:T(8,128)S(1)}, f32[32,4,8,256]{3,2,1,0:T(8,128)}, u32[]{:S(2)}) %copy-start.1) | copy-done | bytes 1048600
  3.1 0.0 copy-start.2
  3.1 1.2 %copy-done.2 = f32[32,4,8,256]{3,2,1,0:T(8,128)S(1)} copy-done((f32[32,4,8,256]{3,2,1,0:T(8,128)S(1)}, f32[32,4,8,256]{3,2,1,0:T(8,128)}, u32[]{:S(2)}) %copy-start.2) | copy-done | bytes 1048600
  4.3 0.0 copy-start.3
  4.3 0.8 %copy-done.3 = s32[4,8,256]{2,1,0:T(8,128)S(1)} copy-done((s32[4,8,256]{2,1,0:T(8,128)S(1)}, s32[4,8,256]{2,1,0:T(8,128)}, u32[]{:S(2)}) %copy-start.3) | copy-done | bytes 32792
  5.1 0.0 copy-start.4
  5.1 0.7 %copy-done.4 = f32[32,128]{1,0:T(8,128)S(1)} copy-done((f32[32,128]{1,0:T(8,128)S(1)}, f32[32,128]{1,0:T(8,128)}, u32[]{:S(2)}) %copy-start.4) | copy-done | bytes 16408
  5.8 0.0 copy-start.5
  5.8 0.7 %copy-done.5 = s32[4,8]{1,0:T(4,128)S(1)} copy-done((s32[4,8]{1,0:T(4,128)S(1)}, s32[4,8]{1,0:T(4,128)}, u32[]{:S(2)}) %copy-start.5) | copy-done | bytes 152
  6.5 21.0 %solve.1 = (f32[2,4,32,8,256]{4,3,2,1,0:T(8,128)S(1)}, f32[4,32,8,256]{3,2,1,0:T(8,128)S(1)}, f32[4,32,8,256]{3,2,1,0:T(8,128)S(1)}, f32[32,8,128]{2,1,0:T(8,128)S(1)}) custom-call(f32[33,4,8,256]{3,2,1,0:T(8,128)S(1)} %copy-done, f32[32,4,8,256]{3,2,1,0:T(8,128)S(1)} %copy-done.1, f32[32,4,8,256]{3,2,1,0:T(8,128)S(1)} %copy-done.2, ...), custom_call_target="tpu_custom_call" | custom-call | tf_op jit(solution)/shard_map/solve/pallas_call | solution.py:290
  27.5 2.5 %finish.1 = (f32[2,32,4,8,256]{4,3,2,1,0:T(8,128)}, f32[2,32,4,8,256]{4,3,2,1,0:T(8,128)}, f32[32,4,8,256]{3,2,1,0:T(8,128)}) custom-call(f32[2,4,32,8,256]{4,3,2,1,0:T(8,128)S(1)} %get-tuple-element.7.state_buffer, f32[4,32,8,256]{3,2,1,0:T(8,128)S(1)} %get-tuple-element.8.packed, f32[4,32,8,256]{3,2,1,0:T(8,128)S(1)} %get-tuple-element.9.gradient, ...), custom_call_target="tpu_custom_call" | custom-call | tf_op jit(solution)/shard_map/finish/pallas_call | solution.py:383
Async XLA Ops:
  0.6 1.2 %copy-start = (f32[33,4,8,256]{3,2,1,0:T(8,128)S(1)}, f32[33,4,8,256]{3,2,1,0:T(8,128)}, u32[]{:S(2)}) copy-start(f32[33,4,8,256]{3,2,1,0:T(8,128)} %state.1) | copy-start | bytes 3244036
  1.9 1.2 %copy-start.1 = (f32[32,4,8,256]{3,2,1,0:T(8,128)S(1)}, f32[32,4,8,256]{3,2,1,0:T(8,128)}, u32[]{:S(2)}) copy-start(f32[32,4,8,256]{3,2,1,0:T(8,128)} %adjoint.1) | copy-start | bytes 3145732
  3.1 1.2 %copy-start.2 = (f32[32,4,8,256]{3,2,1,0:T(8,128)S(1)}, f32[32,4,8,256]{3,2,1,0:T(8,128)}, u32[]{:S(2)}) copy-start(f32[32,4,8,256]{3,2,1,0:T(8,128)} %control.1) | copy-start | bytes 3145732
  4.3 0.8 %copy-start.3 = (s32[4,8,256]{2,1,0:T(8,128)S(1)}, s32[4,8,256]{2,1,0:T(8,128)}, u32[]{:S(2)}) copy-start(s32[4,8,256]{2,1,0:T(8,128)} %labels.1) | copy-start | bytes 98308
  5.1 0.7 %copy-start.4 = (f32[32,128]{1,0:T(8,128)S(1)}, f32[32,128]{1,0:T(8,128)}, u32[]{:S(2)}) copy-start(f32[32,128]{1,0:T(8,128)} %target.1) | copy-start | bytes 49156
  5.8 0.7 %copy-start.5 = (s32[4,8]{1,0:T(4,128)S(1)}, s32[4,8]{1,0:T(4,128)}, u32[]{:S(2)}) copy-start(s32[4,8]{1,0:T(4,128)} %mask.1) | copy-start | bytes 388

commit v3 on v2

--- a/solution.py
+++ b/solution.py
@@ -11,7 +11,7 @@
 time_step = 0.15
 penalty = 0.5
 MESH = pl.DeviceIdType.MESH
-ANY = pl.BlockSpec(memory_space=pl.ANY)
+HBM = pl.BlockSpec(memory_space=pltpu.HBM)
 
 
 def real_transform(values):
@@ -59,9 +59,9 @@
 
 def solve_kernel(
     count, state, adjoint, control, regions, target, mask,
-    state_buffer, packed, gradient, table,
-    sampled, held, multipliers, heat, labels, residual, partial, paired, summed, gathered,
-    label_sem, sample_sem, held_sem, mult_sem, heat_sem,
+    state_buffer, packed, gradient, table, labels,
+    sampled, held, multipliers, heat, wanted, allowed, residual, partial, paired, summed, gathered,
+    small_sem, sample_sem, held_sem, mult_sem, heat_sem,
     halo_send, halo_recv, pair_send, pair_recv, peer_send, peer_recv,
 ):
     steps, rows, planes, width = control.shape
@@ -78,12 +78,16 @@
     for other in [above, below] + peers:
         pl.semaphore_signal(barrier, inc=1, device_id={"space": other}, device_id_type=MESH)
 
-    sums_loads = [pltpu.make_async_copy(regions, labels, label_sem.at[0])] + [
+    sums_loads = [pltpu.make_async_copy(regions, labels, small_sem.at[0])] + [
         pltpu.make_async_copy(
             state.at[pl.ds(1, steps), :, :, pl.ds(block * 128, 128)],
             sampled.at[block], sample_sem.at[block],
         )
         for block in range(blocks)
+    ]
+    small_loads = [
+        pltpu.make_async_copy(target, wanted, small_sem.at[1]),
+        pltpu.make_async_copy(mask, allowed, small_sem.at[2]),
     ]
     heat_loads, mult_loads, held_loads = [], [], []
     for y in range(rows):
@@ -94,7 +98,7 @@
         held_loads.append(
             pltpu.make_async_copy(state.at[pl.ds(0, steps + 1), y], held.at[y + 1], held_sem.at[y])
         )
-    for load in sums_loads + heat_loads + mult_loads + held_loads:
+    for load in sums_loads + small_loads + heat_loads + mult_loads + held_loads:
         load.start()
 
     copies = []
@@ -168,10 +172,10 @@
     def support_of(y):
         support = jnp.zeros((planes, width), jnp.float32)
         for plane in range(planes):
-            support = jnp.where(plane_ids == plane, mask[y, plane].astype(jnp.float32), support)
+            support = jnp.where(plane_ids == plane, allowed[y, plane].astype(jnp.float32), support)
         return support
 
-    for load in heat_loads + mult_loads:
+    for load in small_loads + heat_loads + mult_loads:
         load.wait()
 
     def gradient_row(y, carry):
@@ -257,7 +261,7 @@
     for d, send in enumerate(sends):
         send.wait()
         result = result + gathered[d]
-    misfit = result[:steps] / result[steps : steps + 1] - target[...]
+    misfit = result[:steps] / result[steps : steps + 1] - wanted[...]
     values = real_transform(
         [jnp.broadcast_to(misfit[j : j + 1], (8, count_regions)) for j in range(steps)]
     )
@@ -294,21 +298,23 @@
             vmem((rows, steps, planes, width), f32),
             vmem((rows, steps, planes, width), f32),
             vmem((steps, 8, count_regions), f32),
+            vmem(regions.shape, jnp.int32),
         ),
-        in_specs=[ANY] * 4 + [in_vmem, pl.BlockSpec(memory_space=pltpu.SMEM)],
-        out_specs=(in_vmem,) * 4,
+        in_specs=[HBM] * 6,
+        out_specs=(in_vmem,) * 5,
         scratch_shapes=[
             vmem((blocks, steps, rows, planes, 128), f32),
             vmem((rows + 2, steps + 1, planes, width), f32),
             vmem((rows + 2, steps, planes, width), f32),
             vmem((rows, steps, planes, width), f32),
-            vmem(regions.shape, jnp.int32),
+            vmem(target.shape, f32),
+            pltpu.SMEM(mask.shape, jnp.int32),
             vmem((steps, planes, width), f32),
             vmem(padded, f32),
             vmem(padded, f32),
             vmem(padded, f32),
             vmem((half - 1,) + padded, f32),
-            dma((1,)),
+            dma((3,)),
             dma((blocks,)),
             dma((rows,)),
             dma((rows,)),
@@ -375,7 +381,7 @@
         copy.wait()
 
 
-def finish(control, state_buffer, packed, gradient, table, regions):
+def finish(control, state_buffer, packed, gradient, table, labels):
     steps, rows, planes, width = control.shape
     f32, dma = jnp.float32, pltpu.SemaphoreType.DMA
     in_vmem = pl.BlockSpec(memory_space=pltpu.VMEM)
@@ -384,7 +390,7 @@
         finish_kernel,
         out_shape=(spectrum_shape, spectrum_shape, jax.ShapeDtypeStruct(control.shape, f32)),
         in_specs=[in_vmem] * 5,
-        out_specs=(ANY,) * 3,
+        out_specs=(HBM,) * 3,
         scratch_shapes=[
             pltpu.VMEM((2, rows, steps, planes, width), f32),
             dma((2, rows)),
@@ -393,12 +399,15 @@
         ],
         compiler_params=pltpu.CompilerParams(vmem_limit_bytes=16 * 2**20),
         name="finish",
-    )(state_buffer, packed, gradient, table, regions)
-
-
-def on_device(count, state, adjoint, control, target, mask, regions):
+    )(state_buffer, packed, gradient, table, labels)
+
+
+def on_device(count, *arrays):
+    state, adjoint, control, target, mask, regions = (
+        pltpu.with_memory_space_constraint(array, pltpu.HBM) for array in arrays
+    )
     found = solve(count, state, adjoint, control, regions, target, mask)
-    return finish(control, *found, regions)
+    return finish(control, *found)
 
 
 def solution(mesh):

time: 30.4 us -> 24.4 us (0.80)
  local copies, waits for them, and re-layouts: 5.83 us -> 0 us
    unnamed x12 -> x0, local copies, waits for them, and re-layouts: 5.83 us -> none
where the time goes in v3:
time: 24.4 us; the launch traced here: 24.2 us
  Pallas kernels  23.6 us (97%)
  between operations  0.64 us (3%)
    pallas_call x1, Pallas kernels, solve(): pl.pallas_call(functools.partial(solve_kernel, count), out_shape=(vmem((2...  21.1 us
    pallas_call x1, Pallas kernels, finish(): pl.pallas_call(finish_kernel, out_shape=(spectrum_shape, spectrum_shape,...  2.49 us

profile of v3, /device:TPU:1, one launch (start us, length us, event | category | flops | bytes accessed | tf_op | source)
XLA Modules:
  0.0 24.2 jit_solution(3999735636282666954)
XLA Ops:
  0.6 21.1 %solve.1 = (f32[2,4,32,8,256]{4,3,2,1,0:T(8,128)S(1)}, f32[4,32,8,256]{3,2,1,0:T(8,128)S(1)}, f32[4,32,8,256]{3,2,1,0:T(8,128)S(1)}, f32[32,8,128]{2,1,0:T(8,128)S(1)}, s32[4,8,256]{2,1,0:T(8,128)S(1)}) custom-call(f32[33,4,8,256]{3,2,1,0:T(8,128)} %state.1, f32[32,4,8,256]{3,2,1,0:T(8,128)} %adjoint.1, f32[32,4,8,256]{3,2,1,0:T(8,128)} %control.1, ...), custom_call_target="tpu_custom_call" | custom-call | tf_op jit(solution)/shard_map/solve/pallas_call | solution.py:294
  21.7 2.5 %finish.1 = (f32[2,32,4,8,256]{4,3,2,1,0:T(8,128)}, f32[2,32,4,8,256]{4,3,2,1,0:T(8,128)}, f32[32,4,8,256]{3,2,1,0:T(8,128)}) custom-call(f32[2,4,32,8,256]{4,3,2,1,0:T(8,128)S(1)} %get-tuple-element.8.state_buffer, f32[4,32,8,256]{3,2,1,0:T(8,128)S(1)} %get-tuple-element.9.packed, f32[4,32,8,256]{3,2,1,0:T(8,128)S(1)} %get-tuple-element.10.gradient, ...), custom_call_target="tpu_custom_call" | custom-call | tf_op jit(solution)/shard_map/finish/pallas_call | solution.py:389

commit v4 on v3

--- a/solution.py
+++ b/solution.py
@@ -60,23 +60,31 @@
 def solve_kernel(
     count, state, adjoint, control, regions, target, mask,
     state_buffer, packed, gradient, table, labels,
-    sampled, held, multipliers, heat, wanted, allowed, residual, partial, paired, summed, gathered,
+    sampled, held, multipliers, heat, wanted, allowed, residual, partial, paired, joined, crossed, summed, from_lower, from_upper, to_upper, to_lower,
     small_sem, sample_sem, held_sem, mult_sem, heat_sem,
-    halo_send, halo_recv, pair_send, pair_recv, peer_send, peer_recv,
+    halo_send, halo_recv, pair_send, pair_recv, chain_send, chain_recv,
 ):
     steps, rows, planes, width = control.shape
     count_regions = target.shape[1]
     blocks = width // 128
-    half = count // 2
+    links = count // 4
     me = lax.axis_index("space")
-    group, core = me // 2, me % 2
+    link, place = me // 4, me % 4
     above, below = (me + 1) % count, (me + count - 1) % count
-    partner = group * 2 + 1 - core
-    peers = [((group + d) % half) * 2 + core for d in range(1, half)]
+    partner = (me // 2) * 2 + 1 - me % 2
+    across = link * 4 + (place + 2) % 4
+    upper, lower = (me + 4) % count, (me + count - 4) % count
+    has_upper, has_lower = link < links - 1, link > 0
 
     barrier = pltpu.get_barrier_semaphore()
-    for other in [above, below] + peers:
+
+    def greet(other):
         pl.semaphore_signal(barrier, inc=1, device_id={"space": other}, device_id_type=MESH)
+
+    for other in (above, below, across):
+        greet(other)
+    pl.when(has_upper)(lambda: greet(upper))
+    pl.when(has_lower)(lambda: greet(lower))
 
     sums_loads = [pltpu.make_async_copy(regions, labels, small_sem.at[0])] + [
         pltpu.make_async_copy(
@@ -147,15 +155,14 @@
             stacked, onehot, (((1,), (1,)), ((), ())), preferred_element_type=jnp.float32
         )
 
+    greeted = 3 + has_upper.astype(jnp.int32) + has_lower.astype(jnp.int32)
+    pl.semaphore_wait(barrier, greeted)
+    for copy in copies[:2]:
+        copy.start()
     for load in sums_loads:
         load.wait()
-    early = rows // 2
     total = jnp.zeros((2 * steps + 16, count_regions), jnp.float32)
-    total = lax.fori_loop(0, early, add_row, total)
-    pl.semaphore_wait(barrier, 1 + half)
-    for copy in copies[:2]:
-        copy.start()
-    total = lax.fori_loop(early, rows, add_row, total)
+    total = lax.fori_loop(0, rows, add_row, total)
     partial[:steps] = total[:steps] + total[steps : 2 * steps]
     partial[steps:] = total[2 * steps : 2 * steps + 8]
     pair = pltpu.make_async_remote_copy(
@@ -190,18 +197,43 @@
     lax.fori_loop(0, rows, gradient_row, 0)
 
     pair.wait()
-    summed[...] = partial[...] + paired[...]
-    sends = [
-        pltpu.make_async_remote_copy(
-            src_ref=summed, dst_ref=gathered.at[d], send_sem=peer_send.at[d], recv_sem=peer_recv.at[d],
-            device_id={"space": peer}, device_id_type=MESH,
-        )
-        for d, peer in enumerate(peers)
-    ]
-    for send in sends:
-        send.start()
-    for copy in copies[2:]:
+    joined[...] = partial[...] + paired[...]
+    cross = pltpu.make_async_remote_copy(
+        src_ref=joined, dst_ref=crossed, send_sem=pair_send.at[1], recv_sem=pair_recv.at[1],
+        device_id={"space": across}, device_id_type=MESH,
+    )
+    cross.start()
+    for copy in copies[2:4]:
         copy.start()
+
+    upward = pltpu.make_async_remote_copy(
+        src_ref=to_upper, dst_ref=from_lower, send_sem=chain_send.at[0], recv_sem=chain_recv.at[0],
+        device_id={"space": upper}, device_id_type=MESH,
+    )
+    downward = pltpu.make_async_remote_copy(
+        src_ref=to_lower, dst_ref=from_upper, send_sem=chain_send.at[1], recv_sem=chain_recv.at[1],
+        device_id={"space": lower}, device_id_type=MESH,
+    )
+
+    def pass_on(copy, arriving, leaving, has_source, has_target):
+        pl.when(has_source)(copy.wait_recv)
+
+        @pl.when(jnp.logical_not(has_source))
+        def _():
+            arriving[...] = jnp.zeros_like(arriving)
+
+        @pl.when(has_target)
+        def _():
+            leaving[...] = arriving[...] + summed[...]
+            copy.start()
+
+    def pass_up():
+        pass_on(upward, from_lower, to_upper, has_lower, has_upper)
+
+    def pass_down():
+        pass_on(downward, from_upper, to_lower, has_upper, has_lower)
+
+    near_bottom = link < links // 2
 
     def laplace(values, beside):
         total = beside + jnp.where(first_lane, 0.0, pltpu.roll(values, 1, 1))
@@ -249,7 +281,15 @@
         return carry
 
     lax.fori_loop(1, rows - 1, adjoint_inner, 0)
+    cross.wait()
+    summed[...] = joined[...] + crossed[...]
+    pl.when(near_bottom)(pass_up)
+    pl.when(jnp.logical_not(near_bottom))(pass_down)
+    for copy in copies[4:]:
+        copy.start()
     lax.fori_loop(0, 2, adjoint_edge, 0)
+    pl.when(near_bottom)(pass_down)
+    pl.when(jnp.logical_not(near_bottom))(pass_up)
     for load in held_loads:
         load.wait()
     lax.fori_loop(1, rows - 1, state_row, 0)
@@ -257,10 +297,9 @@
         copy.wait()
     lax.fori_loop(0, 2, lambda side, carry: state_row(side * (rows - 1), carry), 0)
 
-    result = summed[...]
-    for d, send in enumerate(sends):
-        send.wait()
-        result = result + gathered[d]
+    result = summed[...] + from_lower[...] + from_upper[...]
+    pl.when(has_upper)(upward.wait_send)
+    pl.when(has_lower)(downward.wait_send)
     misfit = result[:steps] / result[steps : steps + 1] - wanted[...]
     values = real_transform(
         [jnp.broadcast_to(misfit[j : j + 1], (8, count_regions)) for j in range(steps)]
@@ -288,7 +327,7 @@
     steps, rows, planes, width = control.shape
     count_regions = target.shape[1]
     padded = (steps + 8, count_regions)
-    half, blocks = count // 2, width // 128
+    blocks = width // 128
     f32, dma, vmem = jnp.float32, pltpu.SemaphoreType.DMA, pltpu.VMEM
     in_vmem = pl.BlockSpec(memory_space=pltpu.VMEM)
     return pl.pallas_call(
@@ -310,10 +349,9 @@
             vmem(target.shape, f32),
             pltpu.SMEM(mask.shape, jnp.int32),
             vmem((steps, planes, width), f32),
-            vmem(padded, f32),
-            vmem(padded, f32),
-            vmem(padded, f32),
-            vmem((half - 1,) + padded, f32),
+        ]
+        + [vmem(padded, f32)] * 9
+        + [
             dma((3,)),
             dma((blocks,)),
             dma((rows,)),
@@ -321,10 +359,10 @@
             dma((rows,)),
             dma((4 * blocks,)),
             dma((4 * blocks,)),
-            dma((1,)),
-            dma((1,)),
-            dma((half - 1,)),
-            dma((half - 1,)),
+            dma((2,)),
+            dma((2,)),
+            dma((2,)),
+            dma((2,)),
         ],
         compiler_params=pltpu.CompilerParams(
             collective_id=0, has_side_effects=True, vmem_limit_bytes=24 * 2**20

time: 24.4 us -> 26.2 us (1.074)
  the two profiles are of different devices: /device:TPU:1 before, /device:TPU:0 now
where the time goes in v4:
time: 26.2 us; the launch traced here: 26.1 us
  Pallas kernels  25.4 us (97%)
  between operations  0.64 us (2%)
    pallas_call x1, Pallas kernels, solve(): pl.pallas_call(functools.partial(solve_kernel, count), out_shape=(vmem((2...  23 us
    pallas_call x1, Pallas kernels, finish(): pl.pallas_call(finish_kernel, out_shape=(spectrum_shape, spectrum_shape,...  2.49 us

profile of v4, /device:TPU:0, one launch (start us, length us, event | category | flops | bytes accessed | tf_op | source)
XLA Modules:
  0.0 26.1 jit_solution(10541575956970767229)
XLA Ops:
  0.6 23.0 %solve.1 = (f32[2,4,32,8,256]{4,3,2,1,0:T(8,128)S(1)}, f32[4,32,8,256]{3,2,1,0:T(8,128)S(1)}, f32[4,32,8,256]{3,2,1,0:T(8,128)S(1)}, f32[32,8,128]{2,1,0:T(8,128)S(1)}, s32[4,8,256]{2,1,0:T(8,128)S(1)}) custom-call(f32[33,4,8,256]{3,2,1,0:T(8,128)} %state.1, f32[32,4,8,256]{3,2,1,0:T(8,128)} %adjoint.1, f32[32,4,8,256]{3,2,1,0:T(8,128)} %control.1, ...), custom_call_target="tpu_custom_call" | custom-call | tf_op jit(solution)/shard_map/solve/pallas_call | solution.py:333
  23.6 2.5 %finish.1 = (f32[2,32,4,8,256]{4,3,2,1,0:T(8,128)}, f32[2,32,4,8,256]{4,3,2,1,0:T(8,128)}, f32[32,4,8,256]{3,2,1,0:T(8,128)}) custom-call(f32[2,4,32,8,256]{4,3,2,1,0:T(8,128)S(1)} %get-tuple-element.8.state_buffer, f32[4,32,8,256]{3,2,1,0:T(8,128)S(1)} %get-tuple-element.9.packed, f32[4,32,8,256]{3,2,1,0:T(8,128)S(1)} %get-tuple-element.10.gradient, ...), custom_call_target="tpu_custom_call" | custom-call | tf_op jit(solution)/shard_map/finish/pallas_call | solution.py:427

commit v5 on v4

--- a/solution.py
+++ b/solution.py
@@ -60,7 +60,7 @@
 def solve_kernel(
     count, state, adjoint, control, regions, target, mask,
     state_buffer, packed, gradient, table, labels,
-    sampled, held, multipliers, heat, wanted, allowed, residual, partial, paired, joined, crossed, summed, from_lower, from_upper, to_upper, to_lower,
+    sampled, held, multipliers, heat, wanted, allowed, residual, partial, paired, joined, crossed, summed, gathered,
     small_sem, sample_sem, held_sem, mult_sem, heat_sem,
     halo_send, halo_recv, pair_send, pair_recv, chain_send, chain_recv,
 ):
@@ -73,18 +73,15 @@
     above, below = (me + 1) % count, (me + count - 1) % count
     partner = (me // 2) * 2 + 1 - me % 2
     across = link * 4 + (place + 2) % 4
-    upper, lower = (me + 4) % count, (me + count - 4) % count
-    has_upper, has_lower = link < links - 1, link > 0
+    peers = [((link + d) % links) * 4 + place for d in range(1, links)]
 
     barrier = pltpu.get_barrier_semaphore()
 
     def greet(other):
         pl.semaphore_signal(barrier, inc=1, device_id={"space": other}, device_id_type=MESH)
 
-    for other in (above, below, across):
+    for other in [above, below, across] + peers:
         greet(other)
-    pl.when(has_upper)(lambda: greet(upper))
-    pl.when(has_lower)(lambda: greet(lower))
 
     sums_loads = [pltpu.make_async_copy(regions, labels, small_sem.at[0])] + [
         pltpu.make_async_copy(
@@ -155,8 +152,7 @@
             stacked, onehot, (((1,), (1,)), ((), ())), preferred_element_type=jnp.float32
         )
 
-    greeted = 3 + has_upper.astype(jnp.int32) + has_lower.astype(jnp.int32)
-    pl.semaphore_wait(barrier, greeted)
+    pl.semaphore_wait(barrier, 3 + len(peers))
     for copy in copies[:2]:
         copy.start()
     for load in sums_loads:
@@ -192,7 +188,7 @@
             gradient[y, j] = penalty * heat[y, j] - support * multipliers[y + 1, j]
             return inner
 
-        return lax.fori_loop(0, steps, step, carry, unroll=8)
+        return lax.fori_loop(0, steps, step, carry, unroll=True)
 
     lax.fori_loop(0, rows, gradient_row, 0)
 
@@ -206,34 +202,13 @@
     for copy in copies[2:4]:
         copy.start()
 
-    upward = pltpu.make_async_remote_copy(
-        src_ref=to_upper, dst_ref=from_lower, send_sem=chain_send.at[0], recv_sem=chain_recv.at[0],
-        device_id={"space": upper}, device_id_type=MESH,
-    )
-    downward = pltpu.make_async_remote_copy(
-        src_ref=to_lower, dst_ref=from_upper, send_sem=chain_send.at[1], recv_sem=chain_recv.at[1],
-        device_id={"space": lower}, device_id_type=MESH,
-    )
-
-    def pass_on(copy, arriving, leaving, has_source, has_target):
-        pl.when(has_source)(copy.wait_recv)
-
-        @pl.when(jnp.logical_not(has_source))
-        def _():
-            arriving[...] = jnp.zeros_like(arriving)
-
-        @pl.when(has_target)
-        def _():
-            leaving[...] = arriving[...] + summed[...]
-            copy.start()
-
-    def pass_up():
-        pass_on(upward, from_lower, to_upper, has_lower, has_upper)
-
-    def pass_down():
-        pass_on(downward, from_upper, to_lower, has_upper, has_lower)
-
-    near_bottom = link < links // 2
+    sends = [
+        pltpu.make_async_remote_copy(
+            src_ref=summed, dst_ref=gathered.at[d], send_sem=chain_send.at[d], recv_sem=chain_recv.at[d],
+            device_id={"space": peer}, device_id_type=MESH,
+        )
+        for d, peer in enumerate(peers)
+    ]
 
     def laplace(values, beside):
         total = beside + jnp.where(first_lane, 0.0, pltpu.roll(values, 1, 1))
@@ -248,7 +223,7 @@
             residual[j] = multipliers[y + 1, j] - later - time_step * laplace(later, beside(j + 1))
             return carry
 
-        lax.fori_loop(0, steps - 1, step, 0, unroll=8)
+        lax.fori_loop(0, steps - 1, step, 0, unroll=True)
         residual[steps - 1] = multipliers[y + 1, steps - 1]
         for block in range(blocks):
             lanes = pl.ds(block * 128, 128)
@@ -273,7 +248,7 @@
             residual[j] = held[y + 1, j + 1] - now - time_step * lap - time_step * support * heat[y, j]
             return inner
 
-        lax.fori_loop(0, steps, step, 0, unroll=8)
+        lax.fori_loop(0, steps, step, 0, unroll=True)
         for block in range(blocks):
             lanes = pl.ds(block * 128, 128)
             real, imag = real_transform([residual[j, :, lanes] for j in range(steps)])
@@ -283,13 +258,11 @@
     lax.fori_loop(1, rows - 1, adjoint_inner, 0)
     cross.wait()
     summed[...] = joined[...] + crossed[...]
-    pl.when(near_bottom)(pass_up)
-    pl.when(jnp.logical_not(near_bottom))(pass_down)
+    for send in sends:
+        send.start()
     for copy in copies[4:]:
         copy.start()
     lax.fori_loop(0, 2, adjoint_edge, 0)
-    pl.when(near_bottom)(pass_down)
-    pl.when(jnp.logical_not(near_bottom))(pass_up)
     for load in held_loads:
         load.wait()
     lax.fori_loop(1, rows - 1, state_row, 0)
@@ -297,9 +270,10 @@
         copy.wait()
     lax.fori_loop(0, 2, lambda side, carry: state_row(side * (rows - 1), carry), 0)
 
-    result = summed[...] + from_lower[...] + from_upper[...]
-    pl.when(has_upper)(upward.wait_send)
-    pl.when(has_lower)(downward.wait_send)
+    result = summed[...]
+    for d, send in enumerate(sends):
+        send.wait()
+        result = result + gathered[d]
     misfit = result[:steps] / result[steps : steps + 1] - wanted[...]
     values = real_transform(
         [jnp.broadcast_to(misfit[j : j + 1], (8, count_regions)) for j in range(steps)]
@@ -350,8 +324,9 @@
             pltpu.SMEM(mask.shape, jnp.int32),
             vmem((steps, planes, width), f32),
         ]
-        + [vmem(padded, f32)] * 9
+        + [vmem(padded, f32)] * 5
         + [
+            vmem((count // 4 - 1,) + padded, f32),
             dma((3,)),
             dma((blocks,)),
             dma((rows,)),
@@ -361,8 +336,8 @@
             dma((4 * blocks,)),
             dma((2,)),
             dma((2,)),
-            dma((2,)),
-            dma((2,)),
+            dma((count // 4 - 1,)),
+            dma((count // 4 - 1,)),
         ],
         compiler_params=pltpu.CompilerParams(
             collective_id=0, has_side_effects=True, vmem_limit_bytes=24 * 2**20

time: 26.2 us -> 22.3 us (0.85)
  the two profiles are of different devices: /device:TPU:0 before, /device:TPU:1 now
where the time goes in v5:
time: 22.3 us; the launch traced here: 22.1 us
  Pallas kernels  21.5 us (96%)
  between operations  0.64 us (3%)
    pallas_call x1, Pallas kernels, solve(): pl.pallas_call(functools.partial(solve_kernel, count), out_shape=(vmem((2...  19 us
    pallas_call x1, Pallas kernels, finish(): pl.pallas_call(finish_kernel, out_shape=(spectrum_shape, spectrum_shape,...  2.49 us

profile of v5, /device:TPU:1, one launch (start us, length us, event | category | flops | bytes accessed | tf_op | source)
XLA Modules:
  0.0 22.1 jit_solution(9588284228323453494)
XLA Ops:
  0.6 19.0 %solve.1 = (f32[2,4,32,8,256]{4,3,2,1,0:T(8,128)S(1)}, f32[4,32,8,256]{3,2,1,0:T(8,128)S(1)}, f32[4,32,8,256]{3,2,1,0:T(8,128)S(1)}, f32[32,8,128]{2,1,0:T(8,128)S(1)}, s32[4,8,256]{2,1,0:T(8,128)S(1)}) custom-call(f32[33,4,8,256]{3,2,1,0:T(8,128)} %state.1, f32[32,4,8,256]{3,2,1,0:T(8,128)} %adjoint.1, f32[32,4,8,256]{3,2,1,0:T(8,128)} %control.1, ...), custom_call_target="tpu_custom_call" | custom-call | tf_op jit(solution)/shard_map/solve/pallas_call | solution.py:307
  19.6 2.5 %finish.1 = (f32[2,32,4,8,256]{4,3,2,1,0:T(8,128)}, f32[2,32,4,8,256]{4,3,2,1,0:T(8,128)}, f32[32,4,8,256]{3,2,1,0:T(8,128)}) custom-call(f32[2,4,32,8,256]{4,3,2,1,0:T(8,128)S(1)} %get-tuple-element.8.state_buffer, f32[4,32,8,256]{3,2,1,0:T(8,128)S(1)} %get-tuple-element.9.packed, f32[4,32,8,256]{3,2,1,0:T(8,128)S(1)} %get-tuple-element.10.gradient, ...), custom_call_target="tpu_custom_call" | custom-call | tf_op jit(solution)/shard_map/finish/pallas_call | solution.py:402

commit v6 on v5

--- a/solution.py
+++ b/solution.py
@@ -62,7 +62,7 @@
     state_buffer, packed, gradient, table, labels,
     sampled, held, multipliers, heat, wanted, allowed, residual, partial, paired, joined, crossed, summed, gathered,
     small_sem, sample_sem, held_sem, mult_sem, heat_sem,
-    halo_send, halo_recv, pair_send, pair_recv, chain_send, chain_recv,
+    halo_send, halo_recv, pair_send, pair_recv, chain_send, chain_recv, known,
 ):
     steps, rows, planes, width = control.shape
     count_regions = target.shape[1]
@@ -80,8 +80,24 @@
     def greet(other):
         pl.semaphore_signal(barrier, inc=1, device_id={"space": other}, device_id_type=MESH)
 
-    for other in [above, below, across] + peers:
+    upper, lower = (me + 4) % count, (me + count - 4) % count
+    has_upper, has_lower = link < links - 1, link > 0
+    beside_count = has_upper.astype(jnp.int32) + has_lower.astype(jnp.int32)
+    for other in (above, below, across):
         greet(other)
+    pl.when(has_upper)(lambda: greet(upper))
+    pl.when(has_lower)(lambda: greet(lower))
+
+    def tell(turn):
+        def to(other):
+            pl.semaphore_signal(
+                known.at[turn], inc=1, device_id={"space": other}, device_id_type=MESH
+            )
+
+        pl.when(has_upper)(lambda: to(upper))
+        pl.when(has_lower)(lambda: to(lower))
+
+    turns = links - 2
 
     sums_loads = [pltpu.make_async_copy(regions, labels, small_sem.at[0])] + [
         pltpu.make_async_copy(
@@ -152,7 +168,9 @@
             stacked, onehot, (((1,), (1,)), ((), ())), preferred_element_type=jnp.float32
         )
 
-    pl.semaphore_wait(barrier, 3 + len(peers))
+    pl.semaphore_wait(barrier, 3 + beside_count)
+    if turns > 0:
+        tell(0)
     for copy in copies[:2]:
         copy.start()
     for load in sums_loads:
@@ -258,6 +276,10 @@
     lax.fori_loop(1, rows - 1, adjoint_inner, 0)
     cross.wait()
     summed[...] = joined[...] + crossed[...]
+    for turn in range(max(turns, 0)):
+        pl.semaphore_wait(known.at[turn], beside_count)
+        if turn + 1 < turns:
+            tell(turn + 1)
     for send in sends:
         send.start()
     for copy in copies[4:]:
@@ -338,6 +360,7 @@
             dma((2,)),
             dma((count // 4 - 1,)),
             dma((count // 4 - 1,)),
+            pltpu.SemaphoreType.REGULAR((max(count // 4 - 2, 1),)),
         ],
         compiler_params=pltpu.CompilerParams(
             collective_id=0, has_side_effects=True, vmem_limit_bytes=24 * 2**20

time: 22.3 us -> 22.6 us (1.013)
  Pallas kernels: 21.5 us -> 21.8 us
    pallas_call x1, Pallas kernels: 19 us -> 19.3 us  [solve(): pl.pallas_call(functools.partial(solve_kernel, count), out_shape=(vmem((2...]
where the time goes in v6:
time: 22.6 us; the launch traced here: 22.4 us
  Pallas kernels  21.8 us (96%)
  between operations  0.64 us (3%)
    pallas_call x1, Pallas kernels, solve(): pl.pallas_call(functools.partial(solve_kernel, count), out_shape=(vmem((2...  19.3 us
    pallas_call x1, Pallas kernels, finish(): pl.pallas_call(finish_kernel, out_shape=(spectrum_shape, spectrum_shape,...  2.49 us

profile of v6, /device:TPU:1, one launch (start us, length us, event | category | flops | bytes accessed | tf_op | source)
XLA Modules:
  0.0 22.4 jit_solution(13678951819904665175)
XLA Ops:
  0.6 19.3 %solve.1 = (f32[2,4,32,8,256]{4,3,2,1,0:T(8,128)S(1)}, f32[4,32,8,256]{3,2,1,0:T(8,128)S(1)}, f32[4,32,8,256]{3,2,1,0:T(8,128)S(1)}, f32[32,8,128]{2,1,0:T(8,128)S(1)}, s32[4,8,256]{2,1,0:T(8,128)S(1)}) custom-call(f32[33,4,8,256]{3,2,1,0:T(8,128)} %state.1, f32[32,4,8,256]{3,2,1,0:T(8,128)} %adjoint.1, f32[32,4,8,256]{3,2,1,0:T(8,128)} %control.1, ...), custom_call_target="tpu_custom_call" | custom-call | tf_op jit(solution)/shard_map/solve/pallas_call | solution.py:329
  19.9 2.5 %finish.1 = (f32[2,32,4,8,256]{4,3,2,1,0:T(8,128)}, f32[2,32,4,8,256]{4,3,2,1,0:T(8,128)}, f32[32,4,8,256]{3,2,1,0:T(8,128)}) custom-call(f32[2,4,32,8,256]{4,3,2,1,0:T(8,128)S(1)} %get-tuple-element.8.state_buffer, f32[4,32,8,256]{3,2,1,0:T(8,128)S(1)} %get-tuple-element.9.packed, f32[4,32,8,256]{3,2,1,0:T(8,128)S(1)} %get-tuple-element.10.gradient, ...), custom_call_target="tpu_custom_call" | custom-call | tf_op jit(solution)/shard_map/finish/pallas_call | solution.py:425
